TPU v7x, 32 devices: a whole 2x2x4 slice. The times are simulated.
32 devices in a mesh: dp: 8 (over z, y), head: 4 (over x, core).
Axes of the slice: x: 2, y: 2, z: 4, core: 2. Of those that a mesh axis runs over, the one named last changes fastest.
Arguments:
- inputs: bfloat16 [8, 1024, 768], P('dp', 'head'), may hold values from -6 to 6
- norm_gains: bfloat16 [2, 768], replicated, may hold values from 0.5 to 1.5
- norm_shifts: bfloat16 [2, 768], replicated, may hold values from -1.75 to 1.75
- w_qkv: bfloat16 [768, 2304], replicated, may hold values from -0.21875 to 0.21875
- qv_bias: bfloat16 [2, 768], replicated, may hold values from -1.75 to 1.75
- w_out: bfloat16 [768, 768], replicated, may hold values from -1.75 to 1.75
- out_biases: bfloat16 [2, 768], replicated, may hold values from -1.75 to 1.75
- w_up: bfloat16 [768, 3072], replicated, may hold values from -0.21875 to 0.21875
- up_bias: bfloat16 [3072], replicated, may hold values from -1.75 to 1.75
- w_down: bfloat16 [3072, 768], replicated, may hold values from -0.21875 to 0.21875
- lengths: int32 [8, 4], P('dp'), may hold values from 0 to 1024, as said below
- d_out: bfloat16 [8, 1024, 768], P('dp', 'head'), may hold values from -8 to 8
Outputs:
- block_out: bfloat16 [8, 1024, 768], P('dp', 'head')
- grad_inputs: float32 [8, 1024, 768], P('dp', 'head')
- grad_norm_gains: float32 [2, 768], P(None, 'dp')
- grad_norm_shifts: float32 [2, 768], P(None, 'dp')
- grad_qkv: float32 [768, 2304], P(None, 'dp')
- grad_qv_bias: float32 [2, 768], P(None, 'dp')
- grad_out: float32 [768, 768], P(None, 'dp')
- grad_out_biases: float32 [2, 768], P(None, 'dp')
- grad_up: float32 [768, 3072], P(None, 'dp')
- grad_up_bias: float32 [3072], P('dp')
- grad_down: float32 [3072, 768], P(None, 'dp')
Inputs may be any that keep to these rules, and one draw needn't show every extreme that they name: Each slot holds either one image of 1024 patches (lengths 1024, then zeros) or 1 to 4 images of 256 patches in its first entries, then zeros. The first slot holds one image of 1024 patches.
All inputs are finite; a program needn't handle non-finite values.
Results may differ from a plain program's by a relative error of at most 0.014.
Values may be sent and summed in bfloat16 or wider, within the bound.
A program may use at most 256 MiB of HBM per device.

v0:
```python
import jax
import jax.numpy as jnp
from jax import lax
from jax.sharding import PartitionSpec as P

D = 768
HEADS = 12
HDIM = 64
SLOT = 1024
ITEMS = 4
EPSILON = 1e-06


def norm_parts(values, norm_gain, norm_shift):
    average = jnp.mean(values, axis=-1, keepdims=True)
    centered = values - average
    variance = jnp.mean(centered * centered, axis=-1, keepdims=True)
    inverse = lax.rsqrt(variance + EPSILON)
    normal_unit = centered * inverse
    return (normal_unit, inverse, normal_unit * norm_gain + norm_shift)


def norm_back(grad_normed, normal_unit, inverse, norm_gain):
    grad_unit = grad_normed * norm_gain
    first_mean = jnp.mean(grad_unit, axis=-1, keepdims=True)
    second_mean = jnp.mean(grad_unit * normal_unit, axis=-1, keepdims=True)
    return inverse * (grad_unit - first_mean - normal_unit * second_mean)


def exact_gelu(values):
    return jax.nn.gelu(values, approximate=False)


def slot_allowed(lengths_row):
    item_ends = jnp.cumsum(lengths_row)
    positions = jnp.arange(SLOT, dtype=jnp.int32)
    segment = jnp.sum((positions[:, None] >= item_ends[None, :]).astype(jnp.int32), axis=1)
    is_real = positions < item_ends[ITEMS - 1]
    same_item = (segment[:, None] == segment[None, :]) & is_real[None, :]
    return (same_item | (positions[:, None] == positions[None, :]))[None]


def block_scores(query_part, key_part, allowed):
    scores = jnp.einsum("hbqe,hbke->hbqk", query_part, key_part, preferred_element_type=jnp.float32)
    scores = scores * query_part.shape[-1] ** (-0.5)
    return jnp.where(allowed[None], scores, -jnp.inf)


def block_forward(query_part, key_part, value_part, allowed):
    masked = block_scores(query_part, key_part, allowed)
    row_max = jnp.max(masked, axis=-1, keepdims=True)
    weights = jnp.exp(masked - row_max)
    row_sum = jnp.sum(weights, axis=-1, keepdims=True)
    low_weights = (weights / row_sum).astype(jnp.bfloat16)
    mixed_out = jnp.einsum(
        "hbqk,hbke->hbqe", low_weights, value_part, preferred_element_type=jnp.float32
    )
    return (mixed_out.astype(jnp.bfloat16), (row_max + jnp.log(row_sum))[..., 0])


def block_backward(query_part, key_part, value_part, allowed, grad_mixed, log_totals):
    masked = block_scores(query_part, key_part, allowed)
    attn_weights = jnp.exp(masked - log_totals[..., None])
    grad_weights = jnp.einsum(
        "hbqe,hbke->hbqk", grad_mixed, value_part, preferred_element_type=jnp.float32
    )
    row_inner = jnp.sum(attn_weights * grad_weights, axis=-1, keepdims=True)
    grad_scores = (attn_weights * (grad_weights - row_inner)).astype(jnp.bfloat16)
    score_scale = query_part.shape[-1] ** (-0.5)
    grad_query = (
        jnp.einsum("hbqk,hbke->hbqe", grad_scores, key_part, preferred_element_type=jnp.float32)
        * score_scale
    )
    grad_key = (
        jnp.einsum("hbqk,hbqe->hbke", grad_scores, query_part, preferred_element_type=jnp.float32)
        * score_scale
    )
    grad_value = jnp.einsum(
        "hbqk,hbqe->hbke",
        attn_weights.astype(jnp.bfloat16),
        grad_mixed,
        preferred_element_type=jnp.float32,
    )
    return jnp.stack([grad_query, grad_key, grad_value]).astype(jnp.bfloat16)


def slot_attend(packed, lengths_row):
    head_count = packed.shape[1]

    def whole_slot(operand):
        blocked = operand.reshape(3, head_count, 1, SLOT, HDIM)
        mixed_out, log_totals = block_forward(
            blocked[0], blocked[1], blocked[2], slot_allowed(lengths_row)
        )
        return (mixed_out.reshape(head_count, SLOT * HDIM), log_totals.reshape(head_count, SLOT))

    return whole_slot(packed)


def slot_attend_back(packed, grad_mixed, log_totals, lengths_row):
    head_count = packed.shape[1]

    def whole_slot(operands):
        blocked = operands[0].reshape(3, head_count, 1, SLOT, HDIM)
        result = block_backward(
            blocked[0],
            blocked[1],
            blocked[2],
            slot_allowed(lengths_row),
            operands[1].reshape(head_count, 1, SLOT, HDIM),
            operands[2].reshape(head_count, 1, SLOT),
        )
        return result.reshape(3, head_count, SLOT * HDIM)

    return whole_slot((packed, grad_mixed, log_totals))


def forward_slot(operands):
    return slot_attend(operands[0], operands[1])


def backward_slot(operands):
    return slot_attend_back(operands[0], operands[1], operands[2], operands[3])


def per_device(
    inputs,
    norm_gains,
    norm_shifts,
    w_qkv,
    qv_bias,
    w_out,
    out_biases,
    w_up,
    up_bias,
    w_down,
    lengths,
    d_out,
):
    groups = lax.axis_size("head")
    group_index = lax.axis_index("head")
    slot_count = inputs.shape[0]
    row_count = inputs.shape[1]
    local_heads = HEADS // groups
    gains = norm_gains.astype(jnp.float32)
    shifts = norm_shifts.astype(jnp.float32)
    biases = out_biases.astype(jnp.float32)
    up_shift = up_bias.astype(jnp.float32)
    query_bias = qv_bias.astype(jnp.float32)
    tokens = inputs.astype(jnp.float32)
    first_unit, first_inverse, first_normed = norm_parts(tokens, gains[0], shifts[0])
    normed_one = first_normed.astype(jnp.bfloat16)
    qkv_weight = w_qkv.reshape(D, 3, groups, local_heads, HDIM)
    full_bias = jnp.stack([query_bias[0], jnp.zeros_like(query_bias[0]), query_bias[1]])
    bias_grid = full_bias.reshape(3, groups, local_heads, HDIM).transpose(1, 0, 2, 3)[
        :, :, :, None, :
    ]
    projected = jnp.einsum(
        "srd,dcghe->sgchre", normed_one, qkv_weight, preferred_element_type=jnp.float32
    )
    packed = (
        (projected + bias_grid)
        .astype(jnp.bfloat16)
        .reshape(slot_count, groups, 3, local_heads, row_count * HDIM)
    )
    heads_side = lax.all_to_all(packed, "head", split_axis=1, concat_axis=4, tiled=True)[:, 0]
    mixed_heads, log_totals = lax.map(forward_slot, (heads_side, lengths))
    mixed_patch = lax.all_to_all(
        mixed_heads[:, None], "head", split_axis=3, concat_axis=1, tiled=True
    )
    mixed_patch = mixed_patch.reshape(slot_count, groups, local_heads, row_count, HDIM)
    out_weight = w_out.reshape(groups, local_heads, HDIM, D)
    attention = jnp.einsum(
        "sghre,ghef->srf", mixed_patch, out_weight, preferred_element_type=jnp.float32
    )
    hidden = (tokens + attention + biases[0]).reshape(-1, D)
    second_unit, second_inverse, second_normed = norm_parts(hidden, gains[1], shifts[1])
    normed_two = second_normed.astype(jnp.bfloat16)
    up_values = jnp.dot(normed_two, w_up, preferred_element_type=jnp.float32) + up_shift
    gelu_values, gelu_back = jax.vjp(exact_gelu, up_values)
    activated = gelu_values.astype(jnp.bfloat16)
    down_values = jnp.dot(activated, w_down, preferred_element_type=jnp.float32)
    block_out = (
        (hidden + down_values + biases[1]).astype(jnp.bfloat16).reshape(slot_count, row_count, D)
    )
    positions = group_index * row_count + jnp.arange(row_count, dtype=jnp.int32)
    totals = jnp.sum(lengths, axis=1)
    is_real = (positions[None, :] < totals[:, None]).astype(jnp.float32)
    grad_block = (d_out.astype(jnp.float32) * is_real[:, :, None]).reshape(-1, D)
    grad_low = grad_block.astype(jnp.bfloat16)
    down_grad = jnp.einsum("tf,td->fd", activated, grad_low, preferred_element_type=jnp.float32)
    grad_activated = jnp.einsum("td,fd->tf", grad_low, w_down, preferred_element_type=jnp.float32)
    grad_up = gelu_back(grad_activated)[0]
    grad_up_low = grad_up.astype(jnp.bfloat16)
    up_grad = jnp.einsum("td,tf->df", normed_two, grad_up_low, preferred_element_type=jnp.float32)
    upb_grad = jnp.sum(grad_up, axis=0)
    grad_normed_two = jnp.einsum("tf,df->td", grad_up_low, w_up, preferred_element_type=jnp.float32)
    grad_hidden = grad_block + norm_back(grad_normed_two, second_unit, second_inverse, gains[1])
    grad_hidden_low = grad_hidden.astype(jnp.bfloat16).reshape(slot_count, row_count, D)
    out_grad = jnp.einsum(
        "sghre,srf->ghef", mixed_patch, grad_hidden_low, preferred_element_type=jnp.float32
    ).reshape(D, D)
    grad_mixed = jnp.einsum(
        "srf,ghef->sghre", grad_hidden_low, out_weight, preferred_element_type=jnp.float32
    )
    grad_mixed = grad_mixed.astype(jnp.bfloat16).reshape(
        slot_count, groups, local_heads, row_count * HDIM
    )
    grad_heads = lax.all_to_all(grad_mixed, "head", split_axis=1, concat_axis=3, tiled=True)[:, 0]
    grad_packed = lax.map(backward_slot, (heads_side, grad_heads, log_totals, lengths))
    grad_patch = lax.all_to_all(
        grad_packed[:, None], "head", split_axis=4, concat_axis=1, tiled=True
    )
    grad_patch = grad_patch.reshape(slot_count, groups, 3, local_heads, row_count, HDIM)
    qkv_grad = jnp.einsum(
        "srd,sgchre->dcghe", normed_one, grad_patch, preferred_element_type=jnp.float32
    ).reshape(D, 3 * D)
    bias_sums = jnp.sum(grad_patch, axis=(0, 4), dtype=jnp.float32)
    bias_rows = bias_sums.transpose(1, 0, 2, 3).reshape(3, D)
    qv_grad = jnp.stack([bias_rows[0], bias_rows[2]])
    grad_normed_one = jnp.einsum(
        "sgchre,dcghe->srd", grad_patch, qkv_weight, preferred_element_type=jnp.float32
    )
    grad_inputs = grad_hidden.reshape(slot_count, row_count, D) + norm_back(
        grad_normed_one, first_unit, first_inverse, gains[0]
    )
    gains_grad = jnp.stack(
        [
            jnp.sum(grad_normed_one * first_unit, axis=(0, 1)),
            jnp.sum(grad_normed_two * second_unit, axis=0),
        ]
    )
    shifts_grad = jnp.stack(
        [jnp.sum(grad_normed_one, axis=(0, 1)), jnp.sum(grad_normed_two, axis=0)]
    )
    outb_grad = jnp.stack([jnp.sum(grad_hidden, axis=0), jnp.sum(grad_block, axis=0)])
    shared = (
        lax.psum_scatter(gains_grad, "dp", scatter_dimension=1, tiled=True),
        lax.psum_scatter(shifts_grad, "dp", scatter_dimension=1, tiled=True),
        lax.psum_scatter(qkv_grad, "dp", scatter_dimension=1, tiled=True),
        lax.psum_scatter(qv_grad, "dp", scatter_dimension=1, tiled=True),
        lax.psum_scatter(out_grad, "dp", scatter_dimension=1, tiled=True),
        lax.psum_scatter(outb_grad, "dp", scatter_dimension=1, tiled=True),
        lax.psum_scatter(up_grad, "dp", scatter_dimension=1, tiled=True),
        lax.psum_scatter(upb_grad, "dp", scatter_dimension=0, tiled=True),
        lax.psum_scatter(down_grad, "dp", scatter_dimension=1, tiled=True),
    )
    summed = (
        lax.psum(shared[0].astype(jnp.bfloat16), "head").astype(jnp.float32),
        lax.psum(shared[1].astype(jnp.bfloat16), "head").astype(jnp.float32),
        lax.psum(shared[2].astype(jnp.bfloat16), "head").astype(jnp.float32),
        lax.psum(shared[3].astype(jnp.bfloat16), "head").astype(jnp.float32),
        lax.psum(shared[4].astype(jnp.bfloat16), "head").astype(jnp.float32),
        lax.psum(shared[5].astype(jnp.bfloat16), "head").astype(jnp.float32),
        lax.psum(shared[6].astype(jnp.bfloat16), "head").astype(jnp.float32),
        lax.psum(shared[7].astype(jnp.bfloat16), "head").astype(jnp.float32),
        lax.psum(shared[8].astype(jnp.bfloat16), "head").astype(jnp.float32),
    )
    return (
        block_out,
        grad_inputs,
        summed[0],
        summed[1],
        summed[2],
        summed[3],
        summed[4],
        summed[5],
        summed[6],
        summed[7],
        summed[8],
    )


def solution(mesh):
    placed = (
        P("dp", "head", None),
        P(),
        P(),
        P(),
        P(),
        P(),
        P(),
        P(),
        P(),
        P(),
        P("dp", None),
        P("dp", "head", None),
    )
    return jax.shard_map(
        per_device,
        mesh=mesh,
        in_specs=placed,
        out_specs=(
            P("dp", "head", None),
            P("dp", "head", None),
            P(None, "dp"),
            P(None, "dp"),
            P(None, "dp"),
            P(None, "dp"),
            P(None, "dp"),
            P(None, "dp"),
            P(None, "dp"),
            P("dp"),
            P(None, "dp"),
        ),
        check_vma=False,
    )
```

profile of v0, /device:TPU:0, one launch (start us, length us, event | category | flops | bytes accessed | tf_op | source)
XLA Modules:
  0.0 1841.9 jit_solution(6899083665494931901)
XLA Ops:
  23.1 4.8 all-to-all-start
  33.0 15.0 all-to-all-done
  68.8 50.4 %copy.160 = bf16[1,1,3,65536]{2,1,0,3:T(2,128)(2,1)} copy(bf16[1,1,3,65536]{3,2,1,0:T(4,128)(2,1)S(1)} %broadcast_in_dim.90) | data formatting | bytes 786432 | tf_op jit(solution)/shard_map/broadcast_in_dim | solution.py:169
  119.7 356.0 %reduce.28 = bf16[65536,3]{1,0:T(8,128)(2,1)} reduce(bf16[65536,1,1,3]{3,2,1,0:T(2,128)(2,1)} %bitcast.161, bf16[]{:T(256)} %broadcast.195), dimensions={1,2}, to_apply=%bitcast.124.reduce_sub_computation | reduce | bytes 786434
  475.7 33.0 %reshape.486 = bf16[4,2,24576]{2,1,0:T(2,128)(2,1)} reshape(bf16[65536,3]{1,0:T(8,128)(2,1)} %reduce.28) | data formatting | bytes 786432
  513.0 6.7 all-to-all-done.1
  519.7 51.9 %reshape.487 = bf16[65536,1,1,3]{3,2,1,0:T(2,128)(2,1)} reshape(bf16[4,2,24576]{2,1,0:T(2,128)(2,1)S(1)} %all-to-all-done.1) | data formatting | bytes 786432
  571.6 61.0 %copy.161 = bf16[1,1,3,65536]{3,2,1,0:T(4,128)(2,1)S(1)} copy(bf16[1,1,3,65536]{2,1,0,3:T(2,128)(2,1)} %bitcast.162) | data formatting | bytes 786432 | tf_op jit(solution)/shard_map/all_to_all | solution.py:168
  636.5 11.8 multiply_convert_fusion.1
  663.7 5.4 all-to-all-done.2
  670.0 6.4 multiply_reduce_fusion
  676.4 10.1 multiply_convert_fusion
  686.5 5.1 fusion.23
  703.5 62.5 %copy.177 = bf16[1,1,3,3,65536]{3,2,1,0,4:T(4,128)(2,1)} copy(bf16[1,1,3,3,65536]{4,3,2,1,0:T(4,128)(2,1)S(1)} %pad_maximum_fusion) | data formatting | bytes 2359296 | tf_op jit(solution)/shard_map/while/body/eval_jaxpr/stack | solution.py:84
  766.0 88.2 %reshape.488 = bf16[4,2,73728]{2,1,0:T(2,128)(2,1)S(1)} reshape(bf16[65536,1,1,3,3]{4,3,2,1,0:T(4,128)(2,1)} %bitcast.126) | data formatting | bytes 2359296
  854.2 18.3 all_to_all.60
  872.5 89.1 %reshape.489 = bf16[65536,1,1,3,3]{4,3,2,1,0:T(4,128)(2,1)} reshape(bf16[4,2,73728]{2,1,0:T(2,128)(2,1)S(1)} %all_to_all.60) | data formatting | bytes 2359296
  961.6 90.3 %copy.178 = bf16[1,1,3,3,4,16384]{5,4,3,2,1,0:T(4,128)(2,1)} copy(bf16[1,1,3,3,4,16384]{3,2,5,4,1,0:T(4,128)(2,1)} %bitcast.30) | data formatting | bytes 2359296 | tf_op jit(solution)/shard_map/all_to_all | solution.py:211
  1061.4 6.6 fusion.43
  1068.8 6.7 fusion.57
  1075.5 5.8 copy.149
  1101.1 89.4 %reduce-scatter.17.cloned.1.call-done = f32[768,288]{0,1:T(8,128)} async-done(((f32[768,2304]{0,1:T(8,128)}), f32[768,288]{0,1:T(8,128)}) %reduce-scatter.17.cloned.1.call-update) | async-done | bytes 884752 | tf_op jit(solution)/shard_map/reduce_scatter | solution.py:240
  1192.4 164.4 %reduce-scatter.21.cloned.1.call-done = f32[768,384]{1,0:T(8,128)} async-done(((f32[768,3072]{1,0:T(8,128)}), f32[768,384]{1,0:T(8,128)}) %reduce-scatter.21.cloned.1.call-update) | async-done | bytes 1179664 | tf_op jit(solution)/shard_map/reduce_scatter | solution.py:244
  1359.0 164.3 %reduce-scatter.23.cloned.1.call-done = f32[3072,96]{0,1:T(8,128)} async-done(((f32[3072,768]{0,1:T(8,128)}), f32[3072,96]{0,1:T(8,128)}) %reduce-scatter.23.cloned.1.call-update) | async-done | bytes 1179664 | tf_op jit(solution)/shard_map/reduce_scatter | solution.py:246
  1525.5 5.1 fusion.27
  1530.6 35.1 %all-reduce = bf16[3072]{0:T(1024)(128)(2,1)S(1)} all-reduce(f32[3072]{0:T(1024)S(1)} %copy-done.33), channel_id=9, replica_groups=mesh['dp'=8,'head'=4] {'dp'}, use_global_device_ids=true, to_apply=%region_36.37.clone | all-reduce | flops 3072 | bytes 18432
  1565.9 21.5 %reduce-scatter.31.cloned.1.call-done = f32[96,2]{1,0:T(8,128)} async-done(((f32[768,2]{1,0:T(8,128)}), f32[96,2]{1,0:T(8,128)}) %reduce-scatter.31.cloned.1.call-update) | async-done | bytes 784
  1589.5 61.9 %reduce-scatter.29.cloned.1.call-done = f32[96,2]{1,0:T(8,128)} async-done(((f32[768,2]{1,0:T(8,128)}), f32[96,2]{1,0:T(8,128)}) %reduce-scatter.29.cloned.1.call-update) | async-done | bytes 784
  1652.2 63.1 %reduce-scatter.27.cloned.1.call-done = f32[96,2]{1,0:T(8,128)} async-done(((f32[768,2]{1,0:T(8,128)}), f32[96,2]{1,0:T(8,128)}) %reduce-scatter.27.cloned.1.call-update) | async-done | bytes 784
  1716.2 63.2 %reduce-scatter.25.cloned.1.call-done = f32[96,2]{1,0:T(8,128)} async-done(((f32[768,2]{1,0:T(8,128)}), f32[96,2]{1,0:T(8,128)}) %reduce-scatter.25.cloned.1.call-update) | async-done | bytes 784
  1780.2 5.7 all-reduce.1
  1788.7 40.3 %all-reduce.5.cloned.1.call-done = (bf16[768,288]{0,1:T(8,128)(2,1)}, bf16[768,96]{0,1:T(8,128)(2,1)}, bf16[768,384]{1,0:T(8,128)(2,1)}, bf16[3072,96]{0,1:T(8,128)(2,1)}) async-done(((bf16[768,288]{0,1:T(8,128)(2,1)}, bf16[768,96]{0,1:T(8,128)(2,1)}, bf16[768,384]{1,0:T(8,128)(2,1)}, bf16[3072,96]{0,1:T(8,128)(2,1)}), (bf16[768,288]{0,1:T(8,128)(2,1)}, bf16[768,96]{0,1:T(8,128)(2,1)}, ...) | async-done | bytes 1769488 | tf_op jit(solution)/shard_map/psum | solution.py:251
  (246 shorter events, 127.5 us)
Async XLA Ops:
  7.2 628.4 %copy-start = (bf16[768,768]{1,0:T(8,128)(2,1)S(1)}, bf16[768,768]{1,0:T(8,128)(2,1)}, u32[]{:S(2)}) copy-start(bf16[768,768]{1,0:T(8,128)(2,1)} %param.17) | copy-start | bytes 3538948
  23.1 24.9 %all-to-all-start = ((bf16[1,4,3,3,16384]{4,3,2,0,1:T(4,128)(2,1)}), bf16[1,4,3,3,16384]{4,3,2,0,1:T(4,128)(2,1)S(1)}, u32[]{:S(2)}, u32[]{:S(2)}) async-start(bf16[1,4,3,3,16384]{4,3,2,0,1:T(4,128)(2,1)} %reshape.468), calls=%async_computation | async-start | bytes 3145728 | tf_op jit(solution)/shard_map/all_to_all | solution.py:166
  508.7 11.1 all-to-all-start.1
  513.0 140.4 %copy-start.24 = (f32[256]{0:T(256)}, f32[256]{0:T(256)S(1)}, u32[]{:S(2)}) copy-start(f32[256]{0:T(256)S(1)} %compare_convert_fusion) | copy-start | bytes 3076
  571.6 64.0 %copy-start.8 = (bf16[1,256,768]{2,1,0:T(8,128)(2,1)S(1)}, bf16[1,256,768]{2,1,0:T(8,128)(2,1)}, u32[]{:S(2)}) copy-start(bf16[1,256,768]{2,1,0:T(8,128)(2,1)} %param.12) | copy-start | bytes 1179652
  635.6 12.8 slice-start.5
  635.6 15.7 slice-start.3
  636.2 17.2 copy-start.6
  636.5 17.0 copy-start.32
  636.5 11.9 copy-start.11
  636.5 11.9 slice-start.6
  636.5 14.7 slice-start.4
  656.7 12.3 all-to-all-start.2
  660.2 439.2 %reduce-scatter.19.cloned.1.call-start = ((), (), s32[]{:S(2)}) async-start(), calls=%async_computation.13 | async-start | bytes 2654208 | tf_op jit(solution)/shard_map/reduce_scatter | solution.py:242
  663.6 526.8 %reduce-scatter.17.cloned.1.call-start = ((), (), s32[]{:S(2)}) async-start(), calls=%async_computation.12 | async-start | bytes 7962624 | tf_op jit(solution)/shard_map/reduce_scatter | solution.py:240
  670.0 23.7 %slice-start = ((s8[12582912]{0:T(1024)(128)(4,1)}), s8[4194304]{0:T(1024)(128)(4,1)S(1)}, s32[]{:S(2)}) async-start(s8[12582912]{0:T(1024)(128)(4,1)} %bitcast.159), calls=%async_computation.21 | async-start | bytes 8388608
  670.0 23.7 %slice-start.1 = ((s8[12582912]{0:T(1024)(128)(4,1)}), s8[4194304]{0:T(1024)(128)(4,1)S(1)}, s32[]{:S(2)}) async-start(s8[12582912]{0:T(1024)(128)(4,1)} %bitcast.159), calls=%async_computation.22 | async-start | bytes 8388608
  676.4 17.3 slice-start.2
  1060.3 296.5 %reduce-scatter.21.cloned.1.call-start = ((), (), s32[]{:S(2)}) async-start(), calls=%async_computation.14 | async-start | bytes 10616832 | tf_op jit(solution)/shard_map/reduce_scatter | solution.py:244
  1068.1 455.2 %reduce-scatter.23.cloned.1.call-start = ((), (), s32[]{:S(2)}) async-start(), calls=%async_computation.15 | async-start | bytes 10616832 | tf_op jit(solution)/shard_map/reduce_scatter | solution.py:246
  1075.5 511.8 %reduce-scatter.31.cloned.1.call-start = ((), (), s32[]{:S(2)}) async-start(), calls=%async_computation.19 | async-start | bytes 442368
  1086.0 565.3 %reduce-scatter.29.cloned.1.call-start = ((), (), s32[]{:S(2)}) async-start(), calls=%async_computation.18 | async-start | bytes 442368
  1095.3 620.1 %reduce-scatter.27.cloned.1.call-start = ((), (), s32[]{:S(2)}) async-start(), calls=%async_computation.17 | async-start | bytes 442368
  1097.0 682.3 %reduce-scatter.25.cloned.1.call-start = ((), (), s32[]{:S(2)}) async-start(), calls=%async_computation.16 | async-start | bytes 442368
  1098.1 730.9 %all-reduce.5.cloned.1.call-start = ((), (), s32[]{:S(2)}) async-start(), calls=%async_computation.20 | async-start | bytes 3538944 | tf_op jit(solution)/shard_map/psum | solution.py:251
  1101.1 424.4 %copy-start.42 = (f32[768]{0:T(1024)S(1)}, f32[768]{0:T(1024)}, u32[]{:S(2)}) copy-start(f32[768]{0:T(1024)} %get-tuple-element.52) | copy-start | bytes 9220
  1525.5 62.7 %copy-start.44 = (f32[256]{0:T(256)S(1)}, f32[256]{0:T(256)}, u32[]{:S(2)}) copy-start(f32[256]{0:T(256)} %get-tuple-element.47) | copy-start | bytes 3076
  1525.5 62.7 %copy-start.5 = (f32[256,768]{1,0:T(8,128)S(1)}, f32[256,768]{1,0:T(8,128)}, u32[]{:S(2)}) copy-start(f32[256,768]{1,0:T(8,128)} %copy-done.4) | copy-start | bytes 2359300
  1525.5 62.7 %copy-start.10 = (bf16[1,256,768]{2,1,0:T(8,128)(2,1)S(1)}, bf16[1,256,768]{2,1,0:T(8,128)(2,1)}, u32[]{:S(2)}) copy-start(bf16[1,256,768]{2,1,0:T(8,128)(2,1)} %param.12) | copy-start | bytes 1179652
  1525.5 62.7 %copy-start.16 = (f32[256,768,1,1,1]{1,0,4,3,2:T(8,128)S(1)}, f32[256,768,1,1,1]{1,0,4,3,2:T(8,128)}, u32[]{:S(2)}) copy-start(f32[256,768,1,1,1]{1,0,4,3,2:T(8,128)} %copy-done.15) | copy-start | bytes 2359300
  1525.5 62.7 %copy-start.40 = (f32[256]{0:T(256)S(1)}, f32[256]{0:T(256)}, u32[]{:S(2)}) copy-start(f32[256]{0:T(256)} %copy-done.38) | copy-start | bytes 3076
  1588.3 246.9 %copy-start.1 = (bf16[768,768]{1,0:T(8,128)(2,1)S(1)}, bf16[768,768]{1,0:T(8,128)(2,1)}, u32[]{:S(2)}) copy-start(bf16[768,768]{1,0:T(8,128)(2,1)} %param.17) | copy-start | bytes 3538948
  (34 other events, 161.3 us)
Sparse Core Ops, SparseCore 0:
  664.5 71.7 reduce-scatter.18
  1060.5 129.9 reduce-scatter.16
  1194.5 162.3 reduce-scatter.20
  1360.7 162.5 reduce-scatter.22
  1526.7 60.5 reduce-scatter.30
  1590.8 60.4 reduce-scatter.28
  1654.9 60.3 reduce-scatter.26
  1718.9 60.3 reduce-scatter.24
  1783.3 45.6 all-reduce.4
where the time goes:
time: 1850 us; the launch traced here: 1840 us
  waiting for transfers between devices  695 us (38%)
  local copies, waits for them, and re-layouts  587 us (32%)
  other arithmetic  401 us (22%)
  matrix products  71 us (4%)
  blocking collectives  59.1 us (3%)
    unnamed x4, other arithmetic  356 us
    unnamed x124, local copies, waits for them, and re-layouts  282 us
    unnamed x13, waiting for transfers between devices  210 us
    reduce_scatter x1, waiting for transfers between devices, per_device(): lax.psum_scatter(up_grad, 'dp', scatter_dimension=1, tiled=True)  164 us
    reduce_scatter x1, waiting for transfers between devices, per_device(): lax.psum_scatter(down_grad, 'dp', scatter_dimension=1, tiled=True)  164 us
    all_to_all x1, local copies, waits for them, and re-layouts, per_device(): lax.all_to_all(grad_packed[:, None], 'head', split_axis=4, concat_axis=1,...  90.3 us
    reduce_scatter x1, waiting for transfers between devices, per_device(): lax.psum_scatter(qkv_grad, 'dp', scatter_dimension=1, tiled=True)  89.4 us
    another operation x4, local copies, waits for them, and re-layouts, block_backward(): return jnp.stack([grad_query, grad_key, grad_value]).astype(jnp.bfloat16)  65.8 us
  transfers between devices with their start and end apart: 12, of which 11 were waited for; matrix products, arithmetic and copies ran while one was open for 24% of the time, Pallas kernels for 0%

commit v1 on v0

--- a/solution.py
+++ b/solution.py
@@ -165,9 +165,10 @@
     )
     heads_side = lax.all_to_all(packed, "head", split_axis=1, concat_axis=4, tiled=True)[:, 0]
     mixed_heads, log_totals = lax.map(forward_slot, (heads_side, lengths))
-    mixed_patch = lax.all_to_all(
-        mixed_heads[:, None], "head", split_axis=3, concat_axis=1, tiled=True
-    )
+    part = mixed_heads[:, None]
+    pieces = jnp.split(part, lax.axis_size("head"), axis=3)
+    received = lax.all_to_all(jnp.stack(pieces), "head", 0, 0)
+    mixed_patch = jnp.concatenate(received, axis=1)
     mixed_patch = mixed_patch.reshape(slot_count, groups, local_heads, row_count, HDIM)
     out_weight = w_out.reshape(groups, local_heads, HDIM, D)
     attention = jnp.einsum(

time: 1850 us -> 1300 us (0.70)
  other arithmetic: 401 us -> 46.5 us
  local copies, waits for them, and re-layouts: 587 us -> 392 us
    unnamed x4 -> x3, other arithmetic: 356 us -> 0.01 us
    unnamed x124 -> x121, local copies, waits for them, and re-layouts: 282 us -> 197 us
    all_to_all x2 -> x1, local copies, waits for them, and re-layouts: 62.3 us -> 1.12 us  [per_device(): received = lax.all_to_all(jnp.stack(pieces), 'head', 0, 0)]
    broadcast_in_dim x2 -> x1, local copies, waits for them, and re-layouts: 51 us -> 1.38 us  [per_device(): part = mixed_heads[:, None]]
  transfers between devices with their start and end apart: 12 -> 12, of which waited for: 11 -> 11; matrix products, arithmetic and copies ran while one was open for 24% -> 34% of each run, Pallas kernels for 0% -> 0%
where the time goes in v1:
time: 1300 us; the launch traced here: 1290 us
  waiting for transfers between devices  696 us (54%)
  local copies, waits for them, and re-layouts  392 us (30%)
  matrix products  70.5 us (5%)
  blocking collectives  59.1 us (5%)
  other arithmetic  46.5 us (4%)
  between operations  15.6 us (1%)
    unnamed x13, waiting for transfers between devices  210 us
    unnamed x121, local copies, waits for them, and re-layouts  197 us
    reduce_scatter x1, waiting for transfers between devices, per_device(): lax.psum_scatter(up_grad, 'dp', scatter_dimension=1, tiled=True)  164 us
    reduce_scatter x1, waiting for transfers between devices, per_device(): lax.psum_scatter(down_grad, 'dp', scatter_dimension=1, tiled=True)  164 us
    all_to_all x1, local copies, waits for them, and re-layouts, per_device(): lax.all_to_all(grad_packed[:, None], 'head', split_axis=4, concat_axis=1,...  90.3 us
    reduce_scatter x1, waiting for transfers between devices, per_device(): lax.psum_scatter(qkv_grad, 'dp', scatter_dimension=1, tiled=True)  89.4 us
    another operation x4, local copies, waits for them, and re-layouts, block_backward(): return jnp.stack([grad_query, grad_key, grad_value]).astype(jnp.bfloat16)  65.8 us
    psum x1, waiting for transfers between devices, per_device(): lax.psum(shared[2].astype(jnp.bfloat16), 'head').astype(jnp.float32)  40.2 us
  transfers between devices with their start and end apart: 12, of which 11 were waited for; matrix products, arithmetic and copies ran while one was open for 34% of the time, Pallas kernels for 0%

profile of v1, /device:TPU:0, one launch (start us, length us, event | category | flops | bytes accessed | tf_op | source)
XLA Modules:
  0.0 1292.9 jit_solution(18240997387236982717)
XLA Ops:
  12.1 3.8 fusion.52
  23.1 4.5 all-to-all-start
  32.7 15.0 %all-to-all-done = bf16[1,4,3,3,16384]{4,3,2,0,1:T(4,128)(2,1)S(1)} async-done(((bf16[1,4,3,3,16384]{4,3,2,0,1:T(4,128)(2,1)}), bf16[1,4,3,3,16384]{4,3,2,0,1:T(4,128)(2,1)S(1)}, u32[]{:S(2)}, u32[]{:S(2)}) %all-to-all-start) | async-done | bytes 1179680 | tf_op jit(solution)/shard_map/all_to_all | solution.py:166
  54.8 4.1 fusion.66
  71.9 3.7 all-to-all-start.1
  76.3 8.1 all-to-all-done.1
  88.2 11.5 multiply_convert_fusion.1
  108.0 3.5 all-to-all-start.2
  115.4 4.9 all-to-all-done.2
  121.3 6.2 multiply_reduce_fusion
  127.5 10.1 multiply_convert_fusion
  137.6 5.1 fusion.23
  154.6 62.5 %copy.141 = bf16[1,1,3,3,65536]{3,2,1,0,4:T(4,128)(2,1)} copy(bf16[1,1,3,3,65536]{4,3,2,1,0:T(4,128)(2,1)S(1)} %pad_maximum_fusion) | data formatting | bytes 2359296 | tf_op jit(solution)/shard_map/while/body/eval_jaxpr/stack | solution.py:84
  217.0 88.2 %reshape.484 = bf16[4,2,73728]{2,1,0:T(2,128)(2,1)S(1)} reshape(bf16[65536,1,1,3,3]{4,3,2,1,0:T(4,128)(2,1)} %bitcast.131) | data formatting | bytes 2359296
  305.2 18.3 %all_to_all.50 = bf16[4,2,73728]{2,1,0:T(2,128)(2,1)S(1)} all-to-all(bf16[4,2,73728]{2,1,0:T(2,128)(2,1)S(1)} %reshape.484), channel_id=1, replica_groups=mesh['dp'=8,'head'=4] {'head'}, dimensions={0} | all-to-all | bytes 2359296 | tf_op jit(solution)/shard_map/all_to_all | solution.py:212
  323.5 89.1 %reshape.485 = bf16[65536,1,1,3,3]{4,3,2,1,0:T(4,128)(2,1)} reshape(bf16[4,2,73728]{2,1,0:T(2,128)(2,1)S(1)} %all_to_all.50) | data formatting | bytes 2359296
  412.6 90.3 %copy.142 = bf16[1,1,3,3,4,16384]{5,4,3,2,1,0:T(4,128)(2,1)} copy(bf16[1,1,3,3,4,16384]{3,2,5,4,1,0:T(4,128)(2,1)} %bitcast.33) | data formatting | bytes 2359296 | tf_op jit(solution)/shard_map/all_to_all | solution.py:212
  512.4 6.6 fusion.43
  519.8 6.7 fusion.57
  526.5 5.8 copy.114
  540.2 4.0 fusion.40
  552.1 89.4 %reduce-scatter.17.cloned.1.call-done = f32[768,288]{0,1:T(8,128)} async-done(((f32[768,2304]{0,1:T(8,128)}), f32[768,288]{0,1:T(8,128)}) %reduce-scatter.17.cloned.1.call-update) | async-done | bytes 884752 | tf_op jit(solution)/shard_map/reduce_scatter | solution.py:241
  643.5 164.4 %reduce-scatter.21.cloned.1.call-done = f32[768,384]{1,0:T(8,128)} async-done(((f32[768,3072]{1,0:T(8,128)}), f32[768,384]{1,0:T(8,128)}) %reduce-scatter.21.cloned.1.call-update) | async-done | bytes 1179664 | tf_op jit(solution)/shard_map/reduce_scatter | solution.py:245
  810.1 164.3 %reduce-scatter.23.cloned.1.call-done = f32[3072,96]{0,1:T(8,128)} async-done(((f32[3072,768]{0,1:T(8,128)}), f32[3072,96]{0,1:T(8,128)}) %reduce-scatter.23.cloned.1.call-update) | async-done | bytes 1179664 | tf_op jit(solution)/shard_map/reduce_scatter | solution.py:247
  976.7 5.1 fusion.27
  981.7 35.1 %all-reduce = bf16[3072]{0:T(1024)(128)(2,1)S(1)} all-reduce(f32[3072]{0:T(1024)S(1)} %copy-done.33), channel_id=9, replica_groups=mesh['dp'=8,'head'=4] {'dp'}, use_global_device_ids=true, to_apply=%region_36.37.clone | all-reduce | flops 3072 | bytes 18432
  1017.0 21.4 %reduce-scatter.31.cloned.1.call-done = f32[96,2]{1,0:T(8,128)} async-done(((f32[768,2]{1,0:T(8,128)}), f32[96,2]{1,0:T(8,128)}) %reduce-scatter.31.cloned.1.call-update) | async-done | bytes 784
  1040.5 61.8 %reduce-scatter.29.cloned.1.call-done = f32[96,2]{1,0:T(8,128)} async-done(((f32[768,2]{1,0:T(8,128)}), f32[96,2]{1,0:T(8,128)}) %reduce-scatter.29.cloned.1.call-update) | async-done | bytes 784
  1103.2 63.2 %reduce-scatter.27.cloned.1.call-done = f32[96,2]{1,0:T(8,128)} async-done(((f32[768,2]{1,0:T(8,128)}), f32[96,2]{1,0:T(8,128)}) %reduce-scatter.27.cloned.1.call-update) | async-done | bytes 784
  1167.2 63.2 %reduce-scatter.25.cloned.1.call-done = f32[96,2]{1,0:T(8,128)} async-done(((f32[768,2]{1,0:T(8,128)}), f32[96,2]{1,0:T(8,128)}) %reduce-scatter.25.cloned.1.call-update) | async-done | bytes 784
  1231.4 5.7 all-reduce.1
  1239.8 40.2 %all-reduce.5.cloned.1.call-done = (bf16[768,288]{0,1:T(8,128)(2,1)}, bf16[768,96]{0,1:T(8,128)(2,1)}, bf16[768,384]{1,0:T(8,128)(2,1)}, bf16[3072,96]{0,1:T(8,128)(2,1)}) async-done(((bf16[768,288]{0,1:T(8,128)(2,1)}, bf16[768,96]{0,1:T(8,128)(2,1)}, bf16[768,384]{1,0:T(8,128)(2,1)}, bf16[3072,96]{0,1:T(8,128)(2,1)}), (bf16[768,288]{0,1:T(8,128)(2,1)}, bf16[768,96]{0,1:T(8,128)(2,1)}, ...) | async-done | bytes 1769488 | tf_op jit(solution)/shard_map/psum | solution.py:252
  (242 shorter events, 111.7 us)
Async XLA Ops:
  7.2 80.0 %copy-start = (bf16[768,768]{1,0:T(8,128)(2,1)S(1)}, bf16[768,768]{1,0:T(8,128)(2,1)}, u32[]{:S(2)}) copy-start(bf16[768,768]{1,0:T(8,128)(2,1)} %param.17) | copy-start | bytes 3538948
  23.1 24.6 %all-to-all-start = ((bf16[1,4,3,3,16384]{4,3,2,0,1:T(4,128)(2,1)}), bf16[1,4,3,3,16384]{4,3,2,0,1:T(4,128)(2,1)S(1)}, u32[]{:S(2)}, u32[]{:S(2)}) async-start(bf16[1,4,3,3,16384]{4,3,2,0,1:T(4,128)(2,1)} %reshape.466), calls=%async_computation | async-start | bytes 3145728 | tf_op jit(solution)/shard_map/all_to_all | solution.py:166
  67.9 19.3 %copy-start.8 = (bf16[1,256,768]{2,1,0:T(8,128)(2,1)S(1)}, bf16[1,256,768]{2,1,0:T(8,128)(2,1)}, u32[]{:S(2)}) copy-start(bf16[1,256,768]{2,1,0:T(8,128)(2,1)} %param.12) | copy-start | bytes 1179652
  71.9 12.5 all-to-all-start.1
  76.2 28.4 %copy-start.24 = (f32[256]{0:T(256)}, f32[256]{0:T(256)S(1)}, u32[]{:S(2)}) copy-start(f32[256]{0:T(256)S(1)} %compare_convert_fusion) | copy-start | bytes 3076
  87.2 12.4 slice-start.5
  87.2 15.3 %slice-start.3 = ((s8[4718592]{0:T(1024)(128)(4,1)}), s8[4194304]{0:T(1024)(128)(4,1)S(1)}, s32[]{:S(2)}) async-start(s8[4718592]{0:T(1024)(128)(4,1)} %bitcast.185), calls=%async_computation.24 | async-start | bytes 8388608
  87.8 16.8 %copy-start.6 = (f32[1,256,768]{2,1,0:T(8,128)}, f32[1,256,768]{2,1,0:T(8,128)S(1)}, u32[]{:S(2)}) copy-start(f32[1,256,768]{2,1,0:T(8,128)S(1)} %get-tuple-element.85) | copy-start | bytes 2359300
  88.1 16.6 %copy-start.32 = (f32[256]{0:T(256)}, f32[256]{0:T(256)S(1)}, u32[]{:S(2)}) copy-start(f32[256]{0:T(256)S(1)} %add_rsqrt_fusion) | copy-start | bytes 3076
  88.1 11.5 copy-start.11
  88.1 11.5 slice-start.6
  88.1 14.3 %slice-start.4 = ((s8[4718592]{0:T(1024)(128)(4,1)}), s8[524288]{0:T(1024)(128)(4,1)S(1)}, s32[]{:S(2)}) async-start(s8[4718592]{0:T(1024)(128)(4,1)} %bitcast.185), calls=%async_computation.25 | async-start | bytes 1048576
  108.0 12.3 all-to-all-start.2
  111.5 439.0 %reduce-scatter.19.cloned.1.call-start = ((), (), s32[]{:S(2)}) async-start(), calls=%async_computation.13 | async-start | bytes 2654208 | tf_op jit(solution)/shard_map/reduce_scatter | solution.py:243
  114.9 526.6 %reduce-scatter.17.cloned.1.call-start = ((), (), s32[]{:S(2)}) async-start(), calls=%async_computation.12 | async-start | bytes 7962624 | tf_op jit(solution)/shard_map/reduce_scatter | solution.py:241
  121.3 23.4 %slice-start = ((s8[12582912]{0:T(1024)(128)(4,1)}), s8[4194304]{0:T(1024)(128)(4,1)S(1)}, s32[]{:S(2)}) async-start(s8[12582912]{0:T(1024)(128)(4,1)} %bitcast.164), calls=%async_computation.21 | async-start | bytes 8388608
  121.3 23.4 %slice-start.1 = ((s8[12582912]{0:T(1024)(128)(4,1)}), s8[4194304]{0:T(1024)(128)(4,1)S(1)}, s32[]{:S(2)}) async-start(s8[12582912]{0:T(1024)(128)(4,1)} %bitcast.164), calls=%async_computation.22 | async-start | bytes 8388608
  127.5 17.3 %slice-start.2 = ((s8[12582912]{0:T(1024)(128)(4,1)}), s8[4194304]{0:T(1024)(128)(4,1)S(1)}, s32[]{:S(2)}) async-start(s8[12582912]{0:T(1024)(128)(4,1)} %bitcast.164), calls=%async_computation.23 | async-start | bytes 8388608
  511.3 296.6 %reduce-scatter.21.cloned.1.call-start = ((), (), s32[]{:S(2)}) async-start(), calls=%async_computation.14 | async-start | bytes 10616832 | tf_op jit(solution)/shard_map/reduce_scatter | solution.py:245
  519.1 455.3 %reduce-scatter.23.cloned.1.call-start = ((), (), s32[]{:S(2)}) async-start(), calls=%async_computation.15 | async-start | bytes 10616832 | tf_op jit(solution)/shard_map/reduce_scatter | solution.py:247
  526.5 511.9 %reduce-scatter.31.cloned.1.call-start = ((), (), s32[]{:S(2)}) async-start(), calls=%async_computation.19 | async-start | bytes 442368
  537.0 565.3 %reduce-scatter.29.cloned.1.call-start = ((), (), s32[]{:S(2)}) async-start(), calls=%async_computation.18 | async-start | bytes 442368
  546.3 620.1 %reduce-scatter.27.cloned.1.call-start = ((), (), s32[]{:S(2)}) async-start(), calls=%async_computation.17 | async-start | bytes 442368
  548.0 682.4 %reduce-scatter.25.cloned.1.call-start = ((), (), s32[]{:S(2)}) async-start(), calls=%async_computation.16 | async-start | bytes 442368
  549.1 731.0 %all-reduce.5.cloned.1.call-start = ((), (), s32[]{:S(2)}) async-start(), calls=%async_computation.20 | async-start | bytes 3538944 | tf_op jit(solution)/shard_map/psum | solution.py:252
  552.1 424.5 %copy-start.42 = (f32[768]{0:T(1024)S(1)}, f32[768]{0:T(1024)}, u32[]{:S(2)}) copy-start(f32[768]{0:T(1024)} %get-tuple-element.52) | copy-start | bytes 9220
  976.6 62.7 %copy-start.44 = (f32[256]{0:T(256)S(1)}, f32[256]{0:T(256)}, u32[]{:S(2)}) copy-start(f32[256]{0:T(256)} %get-tuple-element.47) | copy-start | bytes 3076
  976.6 62.7 %copy-start.5 = (f32[256,768]{1,0:T(8,128)S(1)}, f32[256,768]{1,0:T(8,128)}, u32[]{:S(2)}) copy-start(f32[256,768]{1,0:T(8,128)} %copy-done.4) | copy-start | bytes 2359300
  976.6 62.7 %copy-start.10 = (bf16[1,256,768]{2,1,0:T(8,128)(2,1)S(1)}, bf16[1,256,768]{2,1,0:T(8,128)(2,1)}, u32[]{:S(2)}) copy-start(bf16[1,256,768]{2,1,0:T(8,128)(2,1)} %param.12) | copy-start | bytes 1179652
  976.6 62.7 %copy-start.16 = (f32[256,768,1,1,1]{1,0,4,3,2:T(8,128)S(1)}, f32[256,768,1,1,1]{1,0,4,3,2:T(8,128)}, u32[]{:S(2)}) copy-start(f32[256,768,1,1,1]{1,0,4,3,2:T(8,128)} %copy-done.15) | copy-start | bytes 2359300
  976.6 62.7 %copy-start.40 = (f32[256]{0:T(256)S(1)}, f32[256]{0:T(256)}, u32[]{:S(2)}) copy-start(f32[256]{0:T(256)} %copy-done.38) | copy-start | bytes 3076
  1039.3 246.9 %copy-start.1 = (bf16[768,768]{1,0:T(8,128)(2,1)S(1)}, bf16[768,768]{1,0:T(8,128)(2,1)}, u32[]{:S(2)}) copy-start(bf16[768,768]{1,0:T(8,128)(2,1)} %param.17) | copy-start | bytes 3538948
  (34 other events, 160.4 us)
Sparse Core Ops, SparseCore 0:
  115.8 71.6 reduce-scatter.18
  511.5 130.0 reduce-scatter.16
  645.5 162.3 reduce-scatter.20
  811.8 162.5 reduce-scatter.22
  977.9 60.4 reduce-scatter.30
  1041.8 60.4 reduce-scatter.28
  1105.9 60.4 reduce-scatter.26
  1170.0 60.4 reduce-scatter.24
  1234.4 45.6 all-reduce.4
